TPU v7x, 256 devices: a whole 4x4x8 slice. The times are simulated.
256 devices in a mesh: lev: 2 (over core), wa: 128 (over y, z, x).
Axes of the slice: x: 4, y: 4, z: 8, core: 2. Of those that a mesh axis runs over, the one named last changes fastest.
Arguments:
- spectral: bfloat16 [1280, 1280, 2, 64], P('wa', None, None, 'lev'), parts along dimension 3, may hold values from -0.15625 to 0.15625
- legendre: bfloat16 [1280, 1280, 384], P('wa'), may hold values from -0.15625 to 0.15625
- wavenumber: int32 [1280], P('wa'), may hold values from 0 to 1279, each once
Outputs:
- grid: float32 [768, 2560, 64], P('wa', None, 'lev'), parts along dimension 2
There are 2 independent parts, one for each index of `lev`. A program takes and returns all parts, laid end to end along the dimension named above; an argument that names none is the same for every part. Nothing has to cross between parts.
Inputs may be any that keep to these rules, and one draw needn't show every extreme that they name: wavenumber names every number of 0 to 1279 exactly once; slot k of spectral and legendre belongs to wavenumber[k].
All inputs are finite; a program needn't handle non-finite values.
Results may differ from a plain program's by a relative error of at most 0.0003.
Values sent between devices are 32-bit elements.
A program may use at most 128 MiB of HBM per device.

v0:
```python
import math

import jax
import jax.numpy as jnp
from jax import lax
from jax.sharding import PartitionSpec as P

NLON = 2560


def parity_columns(coeff_rows, offset):
    kept_rows = offset >= 0
    even_rows = jnp.logical_and(kept_rows, offset % 2 == 0)[..., None]
    odd_rows = jnp.logical_and(kept_rows, offset % 2 == 1)[..., None]
    nothing = jnp.zeros_like(coeff_rows)
    return jnp.concatenate(
        [jnp.where(even_rows, coeff_rows, nothing), jnp.where(odd_rows, coeff_rows, nothing)], -1
    )


def legendre_every(legendre, coeff_rows, wavenumber):
    row_index = jnp.arange(legendre.shape[1], dtype=jnp.int32)
    split_terms = parity_columns(coeff_rows, row_index[None, :] - wavenumber[:, None])
    return lax.dot_general(
        legendre, split_terms, (((1,), (1,)), ((0,), (0,))), preferred_element_type=jnp.float32
    )


def band_columns(legendre, coeff_rows, wavenumber):
    sums = legendre_every(legendre, coeff_rows, wavenumber)
    columns = coeff_rows.shape[-1]
    even_sums = sums[..., :columns]
    odd_sums = sums[..., columns:]
    return jnp.concatenate([even_sums + odd_sums, (even_sums - odd_sums)[:, ::-1]], 1)


def synthesis(fourier, slot_order, levels):
    longitude = jnp.arange(NLON, dtype=jnp.int32)
    phase_index = slot_order[:, None] * longitude[None, :] % NLON
    lon_angle = phase_index.astype(jnp.float32) * (2.0 * math.pi / NLON)
    weighting = jnp.where(slot_order == 0, 1.0, 2.0).astype(jnp.float32)[:, None]
    cos_sin = jnp.concatenate([weighting * jnp.cos(lon_angle), -weighting * jnp.sin(lon_angle)], 0)
    stacked = jnp.concatenate([fourier[..., :levels], fourier[..., levels:]], 0)
    gridded = lax.dot_general(
        stacked,
        cos_sin,
        (((0,), (0,)), ((), ())),
        precision=lax.Precision.HIGHEST,
        preferred_element_type=jnp.float32,
    )
    return jnp.transpose(gridded, (0, 2, 1))


def on_device(spectral, legendre, wavenumber):
    slot_count = spectral.shape[0]
    degrees = spectral.shape[1]
    levels = spectral.shape[3]
    coeff_rows = spectral.reshape(slot_count, degrees, 2 * levels)
    devices = lax.axis_size("wa")
    every_wave = lax.all_gather(wavenumber, "wa", axis=0, tiled=True)
    by_device = every_wave.reshape(devices, slot_count)
    middle = slot_count // 2
    pieces = []
    orders = []
    for low_slot, high_slot in ((0, middle), (middle, slot_count)):
        columns = band_columns(
            legendre[low_slot:high_slot],
            coeff_rows[low_slot:high_slot],
            wavenumber[low_slot:high_slot],
        )
        pieces.append(lax.all_to_all(columns, "wa", split_axis=1, concat_axis=0, tiled=True))
        orders.append(by_device[:, low_slot:high_slot].reshape(-1))
    fourier = jnp.concatenate(pieces, 0)
    slot_order = jnp.concatenate(orders, 0)
    return synthesis(fourier, slot_order, levels)


def solution(mesh):
    return jax.shard_map(
        on_device,
        mesh=mesh,
        in_specs=(P("wa", None, None, "lev"), P("wa", None, None), P("wa")),
        out_specs=P("wa", None, "lev"),
        check_vma=False,
    )
```

profile of v0, /device:TPU:1, one launch (start us, length us, event | category | flops | bytes accessed | tf_op | source)
XLA Modules:
  0.0 192.3 jit_solution(5546481819754705998)
XLA Ops:
  0.0 0.8 fusion.54
  0.8 0.1 fusion.45
  0.9 0.1 fusion.40
  1.0 1.5 fusion.52
  2.5 1.6 bitcast_select_fusion.1
  4.1 3.4 %fusion.23 = f32[5,384,128]{1,2,0:T(8,128)S(1)} fusion(bf16[10,1280,384]{2,1,0:T(8,128)(2,1)} %param.4, bf16[5,1280,64]{1,2,0:T(8,128)(2,1)S(1)} %get-tuple-element.27, bf16[5,1280,64]{1,2,0:T(8,128)(2,1)S(1)} %get-tuple-element.28), kind=kOutput, calls=%fused_computation.30 | convolution fusion | flops 632422400 | bytes 7536640 | tf_op jit(solution)/shard_map/dot_general | solution.py:24
  7.5 0.1 slice_add_fusion.1
  7.6 0.4 rev.6
  8.0 1.0 pad_maximum_fusion.1
  9.1 0.0 copy-start.2
  9.1 0.0 copy-start.1
  9.1 2.3 %copy.12 = f32[5,768,64]{2,0,1:T(8,128)S(1)} copy(f32[5,768,64]{1,2,0:T(8,128)} %pad_maximum_fusion.1) | data formatting | bytes 1966080 | tf_op jit(solution)/shard_map/concatenate | solution.py:34
  11.3 2.3 %reshape.158 = f32[128,1,1920]{2,1,0:T(1,128)} reshape(f32[768,5,64]{2,1,0:T(8,128)S(1)} %bitcast.32) | data formatting | bytes 1966080
  13.6 16.8 %all-to-all-start = ((f32[128,1,1920]{2,1,0:T(1,128)}), f32[128,1,1920]{2,1,0:T(1,128)}, u32[]{:S(2)}, u32[]{:S(2)}) async-start(f32[128,1,1920]{2,1,0:T(1,128)} %reshape.158), calls=%async_computation | async-start | bytes 1966080 | tf_op jit(solution)/shard_map/all_to_all | solution.py:71
  30.5 0.0 copy-done.2
  30.5 0.6 dynamic-slice
  31.7 0.0 copy-done.1
  31.7 0.3 dynamic-update-slice
  32.0 32.6 %all-reduce = s32[1280]{0:T(1024)S(1)} all-reduce(s32[1280]{0:T(1024)S(1)} %dynamic-update-slice), channel_id=1, replica_groups=mesh['lev'=2,'wa'=128] {'wa'}, use_global_device_ids=true, to_apply=%add | all-reduce | flops 1280 | bytes 10240
  64.7 0.1 reshape.149
  64.8 0.1 fusion.53
  64.9 0.2 concatenate.42
  65.1 0.2 concatenate.41
  65.3 3.9 %fusion.28 = f32[5,384,128]{1,2,0:T(8,128)S(1)} fusion(bf16[10,1280,384]{2,1,0:T(8,128)(2,1)} %param.4, bf16[5,1280,64]{1,2,0:T(8,128)(2,1)} %get-tuple-element.14, bf16[5,1280,64]{1,2,0:T(8,128)(2,1)} %get-tuple-element.13), kind=kOutput, calls=%fused_computation.31 | convolution fusion | flops 632422400 | bytes 7536640 | tf_op jit(solution)/shard_map/dot_general | solution.py:24
  69.2 0.1 slice_add_fusion
  69.3 0.4 rev.7
  69.7 1.0 pad_maximum_fusion.2
  70.7 2.2 %copy.15 = f32[5,768,64]{2,0,1:T(8,128)S(1)} copy(f32[5,768,64]{1,2,0:T(8,128)} %pad_maximum_fusion.2) | data formatting | bytes 1966080 | tf_op jit(solution)/shard_map/concatenate | solution.py:34
  73.0 2.3 %reshape.156 = f32[128,1,1920]{2,1,0:T(1,128)} reshape(f32[768,5,64]{2,1,0:T(8,128)S(1)} %bitcast.33) | data formatting | bytes 1966080
  75.3 0.0 all-to-all-done
  75.3 9.8 %all-to-all-start.1 = ((f32[128,1,1920]{2,1,0:T(1,128)}), f32[128,1,1920]{2,1,0:T(1,128)}, u32[]{:S(2)}, u32[]{:S(2)}) async-start(f32[128,1,1920]{2,1,0:T(1,128)} %reshape.156), calls=%async_computation.1 | async-start | bytes 1966080 | tf_op jit(solution)/shard_map/all_to_all | solution.py:71
  85.1 57.7 %cosine_multiply_fusion = (f32[1280,2560]{1,0:T(8,128)}, f32[1280,2560]{1,0:T(8,128)}) fusion(s32[1280]{0:T(1024)S(1)} %constant_dynamic-update-slice_fusion, f32[1280]{0:T(1024)S(1)} %get-tuple-element.19, f32[1280]{0:T(1024)S(1)} %get-tuple-element.20), kind=kLoop, calls=%fused_computation.8 | loop fusion | flops 36044800 | bytes 26229760 | tf_op jit(solution)/shard_map/mul | solution.py:42
  142.8 0.5 broadcast.214
  143.3 5.1 %reduce.1 = f32[128,1920]{1,0:T(8,128)} reduce(f32[128,1,1920]{2,1,0:T(1,128)} %all-to-all-done, f32[]{:T(128)} %broadcast.214), dimensions={1}, to_apply=%all_to_all.26.reduce_sub_computation | reduce | bytes 1966084 | tf_op jit(solution)/shard_map/all_to_all | solution.py:71
  148.4 1.8 reshape.159
  150.3 2.0 %copy.14 = f32[128,5,6,64]{3,2,1,0:T(8,128)} copy(f32[128,5,6,64]{3,1,2,0:T(8,128)S(1)} %bitcast.34) | data formatting | bytes 1966080 | tf_op jit(solution)/shard_map/all_to_all | solution.py:71
  152.3 3.0 %copy.18 = f32[640,6,64]{0,2,1:T(8,128)} copy(f32[640,6,64]{2,1,0:T(8,128)} %bitcast.36) | data formatting | bytes 1966080 | tf_op jit(solution)/shard_map/all_to_all | solution.py:71
  155.3 0.0 all-to-all-done.1
  155.3 5.1 %reduce = f32[128,1920]{1,0:T(8,128)} reduce(f32[128,1,1920]{2,1,0:T(1,128)} %all-to-all-done.1, f32[]{:T(128)} %broadcast.214), dimensions={1}, to_apply=%all_to_all.30.reduce_sub_computation | reduce | bytes 1966084 | tf_op jit(solution)/shard_map/all_to_all | solution.py:71
  160.4 1.8 reshape.157
  162.2 2.0 %copy.17 = f32[128,5,6,64]{3,2,1,0:T(8,128)} copy(f32[128,5,6,64]{3,1,2,0:T(8,128)S(1)} %bitcast.35) | data formatting | bytes 1966080 | tf_op jit(solution)/shard_map/all_to_all | solution.py:71
  164.2 0.0 copy-start
  164.2 2.3 %copy.19 = f32[640,6,64]{0,2,1:T(8,128)S(1)} copy(f32[640,6,64]{2,1,0:T(8,128)} %bitcast.37) | data formatting | bytes 1966080 | tf_op jit(solution)/shard_map/all_to_all | solution.py:71
  166.6 1.1 fusion.33
  167.7 0.0 copy-done
  167.7 24.6 %fusion.12 = f32[6,2560,32]{1,2,0:T(8,128)} fusion(f32[1280,2560]{1,0:T(8,128)} %get-tuple-element.18, f32[1280,2560]{1,0:T(8,128)} %get-tuple-element.17, f32[640,6,64]{0,2,1:T(8,128)S(1)} %copy.19, f32[640,6,64]{0,2,1:T(8,128)S(1)} %copy-done, f32[1280,6,32]{0,2,1:T(8,128)S(1)} %fusion.33), kind=kOutput, calls=%fused_computation.17 | convolution fusion | flops 15107031040 | bytes 31129600 | tf_op jit(solution)/shard_map/dot_general | solution.py:44
  (5 shorter events, 0.0 us)
Async XLA Ops:
  9.1 21.4 %copy-start.2 = (u32[256]{0:T(256)S(1)}, u32[256]{0:T(256)}, u32[]{:S(2)}) copy-start(u32[256]{0:T(256)} %constant.53) | copy-start | bytes 3076
  9.1 22.7 %copy-start.1 = (s32[10]{0:T(128)S(1)}, s32[10]{0:T(128)}, u32[]{:S(2)}) copy-start(s32[10]{0:T(128)} %param.5) | copy-start | bytes 124
  13.6 61.7 %all-to-all-start = ((f32[128,1,1920]{2,1,0:T(1,128)}), f32[128,1,1920]{2,1,0:T(1,128)}, u32[]{:S(2)}, u32[]{:S(2)}) async-start(f32[128,1,1920]{2,1,0:T(1,128)} %reshape.158), calls=%async_computation | async-start | bytes 1966080 | tf_op jit(solution)/shard_map/all_to_all | solution.py:71
  75.3 79.9 %all-to-all-start.1 = ((f32[128,1,1920]{2,1,0:T(1,128)}), f32[128,1,1920]{2,1,0:T(1,128)}, u32[]{:S(2)}, u32[]{:S(2)}) async-start(f32[128,1,1920]{2,1,0:T(1,128)} %reshape.156), calls=%async_computation.1 | async-start | bytes 1966080 | tf_op jit(solution)/shard_map/all_to_all | solution.py:71
  164.2 3.5 %copy-start = (f32[640,6,64]{0,2,1:T(8,128)S(1)}, f32[640,6,64]{0,2,1:T(8,128)}, u32[]{:S(2)}) copy-start(f32[640,6,64]{0,2,1:T(8,128)} %copy.18) | copy-start | bytes 2949124
where the time goes:
time: 195 us; the launch traced here: 192 us
  other arithmetic  73 us (37%)
  blocking collectives  32.6 us (17%)
  matrix products  32 us (16%)
  local copies, waits for them, and re-layouts  27.2 us (14%)
  starting transfers between devices  26.6 us (14%)
    mul x1, other arithmetic, synthesis(): weighting * jnp.cos(lon_angle)  57.7 us
    unnamed x1, blocking collectives  32.6 us
    all_to_all x2, starting transfers between devices, on_device(): lax.all_to_all(columns, 'wa', split_axis=1, concat_axis=0, tiled=True)  26.6 us
    dot_general x1, matrix products, synthesis(): lax.dot_general(stacked, cos_sin, (((0,), (0,)), ((), ())), precision=lax...  24.6 us
    all_to_all x2, other arithmetic, on_device(): lax.all_to_all(columns, 'wa', split_axis=1, concat_axis=0, tiled=True)  10.2 us
    all_to_all x5, local copies, waits for them, and re-layouts, on_device(): lax.all_to_all(columns, 'wa', split_axis=1, concat_axis=0, tiled=True)  9.88 us
    unnamed x14, local copies, waits for them, and re-layouts  9.13 us
    dot_general x2, matrix products, legendre_every(): lax.dot_general(legendre, split_terms, (((1,), (1,)), ((0,), (0,))), pref...  7.37 us
  transfers between devices with their start and end apart: 2, of which 0 were waited for; matrix products, arithmetic and copies ran while one was open for 42% of the time, Pallas kernels for 0%

commit v1 on v0

v1 whole, which is shorter than its diff:
```python
import functools
import math

import jax
import jax.numpy as jnp
from jax import lax
from jax.experimental import pallas as pl
from jax.experimental.pallas import tpu as pltpu
from jax.sharding import PartitionSpec as P

NLON = 2560
LANES = 128
MESH = pl.DeviceIdType.MESH


def kernel(
    dims,
    spec_hbm,
    leg_hbm,
    wave_smem,
    out_ref,
    spec,
    leg,
    turned,
    send,
    recv,
    wave_send,
    wave_recv,
    wave_trig,
    table_hi,
    table_lo,
    xs,
    acc,
    spec_sem,
    leg_sem,
    wave_send_sem,
    wave_recv_sem,
    send_sem,
    recv_sem,
):
    devices, slots, degrees, north, columns, rows = dims
    pairs = slots // 2
    half = devices // 2
    levels = columns // 2
    lev = lax.axis_index("lev")
    me = lax.axis_index("wa")

    spec_copy = pltpu.make_async_copy(spec_hbm, spec, spec_sem)
    spec_copy.start()

    def leg_copy(s):
        return pltpu.make_async_copy(leg_hbm.at[pl.ds(2 * s, 2)], leg.at[pl.ds(2 * s, 2)], leg_sem.at[s])

    for s in range(pairs):
        leg_copy(s).start()

    barrier = pltpu.get_barrier_semaphore()

    def greet(i, carry):
        pl.semaphore_signal(barrier, inc=1, device_id=(lev, lax.rem(me + i, devices)), device_id_type=MESH)
        return carry

    lax.fori_loop(1, devices, greet, 0)

    lane_row = lax.broadcasted_iota(jnp.int32, (1, LANES), 1)
    own_waves = jnp.zeros((1, LANES), jnp.float32)
    for k in range(slots):
        own_waves = jnp.where(lane_row == k, wave_smem[k].astype(jnp.float32), own_waves)
    wave_send[...] = own_waves
    wave_recv[me] = own_waves

    spec_copy.wait()
    degree = lax.broadcasted_iota(jnp.int32, (1, degrees), 1)

    def slot_sums(k):
        offset = degree - wave_smem[k]
        kept = jnp.where(offset >= 0, 1.0, 0.0)
        flipped = jnp.where((offset & 1) == 0, kept, -kept)
        rows_in = spec[k].astype(jnp.float32)
        both = jnp.concatenate([rows_in * kept, rows_in * flipped], 0).astype(jnp.bfloat16)
        return jnp.dot(both, leg[k], preferred_element_type=jnp.float32)

    def target(i):
        to = lax.rem(me + i, devices)
        side = jnp.where(to >= half, 1, 0)
        block = jnp.where(to >= half, devices - 1 - to, to)
        return to, side, block

    def make_pair(s):
        leg_copy(s).wait()
        first = slot_sums(2 * s)
        second = slot_sums(2 * s + 1)
        for side in range(2):
            low = side * columns
            stacked = jnp.concatenate([first[low : low + columns], second[low : low + columns]], 0)
            turned[side] = stacked.T
        group = 4

        def pack(g, carry):
            for side in range(2):
                piece = turned[side, pl.ds(pl.multiple_of(g * group * rows, 8), group * rows), :]
                for i in range(group):
                    send[s, side, g * group + i] = piece[i * rows : (i + 1) * rows]
            return carry

        lax.fori_loop(0, half // group, pack, 0)

    def send_pair(s):
        def one(i, carry):
            to, side, block = target(i)
            pltpu.make_async_remote_copy(
                src_ref=send.at[s, side, block],
                dst_ref=recv.at[s, me],
                send_sem=send_sem.at[s],
                recv_sem=recv_sem.at[s],
                device_id=(lev, to),
                device_id_type=MESH,
            ).start()
            return carry

        lax.fori_loop(1, devices, one, 0)
        _, side, block = target(0)
        pltpu.make_async_copy(send.at[s, side, block], recv.at[s, me], recv_sem.at[s]).start()

    make_pair(0)
    pl.semaphore_wait(barrier, devices - 1)

    def send_waves(i, carry):
        pltpu.make_async_remote_copy(
            src_ref=wave_send,
            dst_ref=wave_recv.at[me],
            send_sem=wave_send_sem,
            recv_sem=wave_recv_sem,
            device_id=(lev, lax.rem(me + i, devices)),
            device_id_type=MESH,
        ).start()
        return carry

    lax.fori_loop(1, devices, send_waves, 0)
    send_pair(0)

    def later_pair(s, carry):
        make_pair(s)
        send_pair(s)
        return carry

    lax.fori_loop(1, pairs, later_pair, 0)

    others = pl.ds(0, devices - 1)
    pltpu.make_async_copy(wave_recv.at[others], wave_recv.at[others], wave_recv_sem).wait()

    waves = wave_recv[:, 0, :]
    step_units = waves - 20.0 * jnp.floor((waves + 0.5) * 0.05)
    step_angle = step_units * (2.0 * math.pi / 20.0)
    wave_trig[0] = waves
    wave_trig[1] = jnp.cos(step_angle)
    wave_trig[2] = jnp.sin(step_angle)
    acc[...] = jnp.zeros_like(acc)
    lane_id = lax.broadcasted_iota(jnp.int32, (devices, LANES), 1)
    lane_number = lane_id.astype(jnp.float32)

    def column(which, k):
        picked = jnp.where(lane_id == k, wave_trig[which], 0.0)
        return jnp.broadcast_to(jnp.sum(picked, axis=1, keepdims=True), (devices, LANES))

    def make_tables(s):
        for t in range(2):
            k = 2 * s + t
            wave = column(0, k)
            cos_step = column(1, k)
            sin_step = column(2, k)
            product = wave * lane_number
            turns = jnp.floor(product * (1.0 / NLON) + 0.5)
            angle = (product - turns * NLON) * (2.0 * math.pi / NLON)
            weight = jnp.where(wave == 0.0, 1.0, 2.0)
            cos_part = weight * jnp.cos(angle)
            sin_part = -weight * jnp.sin(angle)
            for q in range(NLON // LANES):
                at = slice(q * LANES, (q + 1) * LANES)
                for p, part in ((0, cos_part), (1, sin_part)):
                    low = (2 * t + p) * devices
                    high_bits = part.astype(jnp.bfloat16)
                    table_hi[low : low + devices, at] = high_bits
                    table_lo[low : low + devices, at] = (part - high_bits.astype(jnp.float32)).astype(jnp.bfloat16)
                cos_part, sin_part = (
                    cos_part * cos_step + sin_part * sin_step,
                    sin_part * cos_step - cos_part * sin_step,
                )

    all_rows = rows * levels

    def use_pair(s):
        for r in range(rows):
            tile = recv[s, :, r, :].T
            high_bits = tile.astype(jnp.bfloat16)
            low_bits = (tile - high_bits.astype(jnp.float32)).astype(jnp.bfloat16)
            at = pl.multiple_of(jnp.where(me >= half, rows - 1 - r, r) * levels, levels)
            for b in range(4):
                piece = slice(b * levels, (b + 1) * levels)
                across = slice(b * devices, (b + 1) * devices)
                xs[pl.ds(at, levels), across] = high_bits[piece]
                xs[pl.ds(at + all_rows, levels), across] = low_bits[piece]
        width = 512

        def block(j, carry):
            at = pl.ds(pl.multiple_of(j * width, width), width)
            main = jnp.dot(xs[...], table_hi[:, at], preferred_element_type=jnp.float32)
            rest = jnp.dot(xs[0:all_rows], table_lo[:, at], preferred_element_type=jnp.float32)
            acc[:, at] += main[0:all_rows] + (main[all_rows:] + rest)
            return carry

        lax.fori_loop(0, NLON // width, block, 0)

    def arrive(s, carry):
        make_tables(s)
        pltpu.make_async_copy(recv.at[s], recv.at[s], recv_sem.at[s]).wait()
        use_pair(s)
        return carry

    lax.fori_loop(0, pairs, arrive, 0)
    out_ref[...] = acc[...]

    def finish(s, carry):
        pltpu.make_async_copy(recv.at[s, others], recv.at[s, others], send_sem.at[s]).wait()
        return carry

    lax.fori_loop(0, pairs, finish, 0)
    pltpu.make_async_copy(wave_recv.at[others], wave_recv.at[others], wave_send_sem).wait()


def solution(mesh):
    devices = mesh.shape["wa"]

    def on_device(spectral, legendre, wavenumber):
        slots, degrees, parts, levels = spectral.shape
        north = legendre.shape[2]
        columns = parts * levels
        rows = 2 * north // devices
        pairs = slots // 2
        spec_rows = jnp.transpose(spectral, (0, 2, 3, 1)).reshape(slots, columns, degrees)
        dims = (devices, slots, degrees, north, columns, rows)
        gridded = pl.pallas_call(
            functools.partial(kernel, dims),
            out_shape=jax.ShapeDtypeStruct((rows * levels, NLON), jnp.float32),
            in_specs=[
                pl.BlockSpec(memory_space=pl.ANY),
                pl.BlockSpec(memory_space=pl.ANY),
                pl.BlockSpec(memory_space=pltpu.SMEM),
            ],
            out_specs=pl.BlockSpec(memory_space=pltpu.VMEM),
            scratch_shapes=[
                pltpu.VMEM((slots, columns, degrees), jnp.bfloat16),
                pltpu.VMEM((slots, degrees, north), jnp.bfloat16),
                pltpu.VMEM((2, north, LANES), jnp.float32),
                pltpu.VMEM((pairs, 2, devices // 2, rows, LANES), jnp.float32),
                pltpu.VMEM((pairs, devices, rows, LANES), jnp.float32),
                pltpu.VMEM((1, LANES), jnp.float32),
                pltpu.VMEM((devices, 1, LANES), jnp.float32),
                pltpu.VMEM((3, devices, LANES), jnp.float32),
                pltpu.VMEM((4 * devices, NLON), jnp.bfloat16),
                pltpu.VMEM((4 * devices, NLON), jnp.bfloat16),
                pltpu.VMEM((2 * rows * levels, 4 * devices), jnp.bfloat16),
                pltpu.VMEM((rows * levels, NLON), jnp.float32),
                pltpu.SemaphoreType.DMA,
                pltpu.SemaphoreType.DMA((pairs,)),
                pltpu.SemaphoreType.DMA,
                pltpu.SemaphoreType.DMA,
                pltpu.SemaphoreType.DMA((pairs,)),
                pltpu.SemaphoreType.DMA((pairs,)),
            ],
            compiler_params=pltpu.CompilerParams(
                collective_id=0, has_side_effects=True, vmem_limit_bytes=60 * 2**20
            ),
        )(spec_rows, legendre, wavenumber)
        return jnp.transpose(gridded.reshape(rows, levels, NLON), (0, 2, 1))

    return jax.shard_map(
        on_device,
        mesh=mesh,
        in_specs=(P("wa", None, None, "lev"), P("wa", None, None), P("wa")),
        out_specs=P("wa", None, "lev"),
        check_vma=False,
    )
```

time: 195 us -> 68.8 us (0.35); the launches traced: 192 us -> 68.7 us
  other arithmetic: 73 us -> 0 us
  Pallas kernels: 0 us -> 65.7 us
  blocking collectives: 32.6 us -> 0 us
  matrix products: 32 us -> 0 us
  starting transfers between devices: 26.6 us -> 0 us
  local copies, waits for them, and re-layouts: 27.2 us -> 2.99 us
    pallas_call x0 -> x1, Pallas kernels: none -> 65.7 us  [on_device(): pl.pallas_call(functools.partial(kernel, dims), out_shape=jax.ShapeDtypeS...]
    mul x1 -> x0, other arithmetic: 57.7 us -> none  [synthesis(): weighting * jnp.cos(lon_angle)]
    unnamed x1 -> x0, blocking collectives: 32.6 us -> none
    dot_general x3 -> x0, matrix products: 32 us -> none  [the longest x1 24.6 us: synthesis(): lax.dot_general(stacked, cos_sin, (((0,), (0,)), ((), ())), precision=lax...]
    all_to_all x2 -> x0, starting transfers between devices: 26.6 us -> none  [on_device(): lax.all_to_all(columns, 'wa', split_axis=1, concat_axis=0, tiled=True)]
    all_to_all x2 -> x0, other arithmetic: 10.2 us -> none  [on_device(): lax.all_to_all(columns, 'wa', split_axis=1, concat_axis=0, tiled=True)]
    all_to_all x5 -> x0, local copies, waits for them, and re-layouts: 9.88 us -> none  [on_device(): lax.all_to_all(columns, 'wa', split_axis=1, concat_axis=0, tiled=True)]
    unnamed x14 -> x1, local copies, waits for them, and re-layouts: 9.13 us -> 2.99 us
  transfers between devices with their start and end apart: 2 -> 0, of which waited for: 0 -> 0; matrix products, arithmetic and copies ran while one was open for 42% -> 0% of each run, Pallas kernels for 0% -> 0%
where the time goes in v1:
time: 68.8 us; the launch traced here: 68.7 us
  Pallas kernels  65.7 us (95%)
  local copies, waits for them, and re-layouts  2.99 us (4%)
    pallas_call x1, Pallas kernels, on_device(): pl.pallas_call(functools.partial(kernel, dims), out_shape=jax.ShapeDtypeS...  65.7 us
    unnamed x1, local copies, waits for them, and re-layouts  2.99 us

profile of v1, /device:TPU:1, one launch (start us, length us, event | category | flops | bytes accessed | tf_op | source)
XLA Modules:
  0.0 68.7 jit_solution(6974729541630515052)
XLA Ops:
  0.0 65.7 %shard_map.37 = f32[192,2560]{1,0:T(8,128)} custom-call(bf16[10,64,1280]{2,1,0:T(8,128)(2,1)} %bitcast.7, bf16[10,1280,384]{2,1,0:T(8,128)(2,1)} %leg_hbm.1, s32[10]{0:T(128)} %wave_smem.1), custom_call_target="tpu_custom_call" | custom-call | tf_op jit(solution)/shard_map/pallas_call | solution.py:242
  65.7 3.0 %copy.5 = f32[6,2560,32]{1,2,0:T(8,128)} copy(f32[6,2560,32]{1,2,0:T(8,128)} %bitcast.6) | data formatting | bytes 3932160

commit v2 on v1

v2 whole, which is shorter than its diff:
```python
import functools
import math

import jax
import jax.numpy as jnp
from jax import lax
from jax.experimental import pallas as pl
from jax.experimental.pallas import tpu as pltpu
from jax.sharding import PartitionSpec as P

NLON = 2560
LANES = 128
MESH = pl.DeviceIdType.MESH
SIZES = (4, 8, 4)


def kernel(
    dims,
    spec_hbm,
    leg_hbm,
    wave_hbm,
    out_ref,
    spec,
    leg,
    turned,
    send,
    recv,
    wave_smem,
    wave_recv,
    wave_trig,
    table_hi,
    table_lo,
    xs,
    wave_sem,
    spec_sem,
    leg_sem,
    line_send_sem,
    line_recv_sem,
    plane_send_sem,
    plane_recv_sem,
    send_sem,
    recv_sem,
):
    sizes, slots, degrees, north, columns, rows = dims
    size_y, size_z, size_x = sizes
    devices = size_y * size_z * size_x
    plane = size_y * size_x
    quarter = size_z // 2
    pairs = slots // 2
    half = devices // 2
    levels = columns // 2
    lev = lax.axis_index("lev")
    me = lax.axis_index("wa")
    my_y = me // (size_z * size_x)
    my_z = lax.rem(me // size_x, size_z)
    my_x = lax.rem(me, size_x)

    def along_z(zslot):
        far, low = zslot // 2, lax.rem(zslot, 2)
        return jnp.where(low == 0, size_z // 2 - far, jnp.where(far == 0, 0, size_z // 2 + far))

    def in_plane(spot):
        dy = lax.rem(size_y // 2 + (size_y - 1) * (spot // size_x), size_y)
        dx = lax.rem(size_x // 2 + (size_x - 1) * lax.rem(spot, size_x), size_x)
        return dy, dx

    def device_at(dz, dy, dx):
        return (
            lax.rem(my_y + dy, size_y) * size_z + lax.rem(my_z + dz, size_z)
        ) * size_x + lax.rem(my_x + dx, size_x)

    own_spot = (size_y // 2) * size_x + size_x // 2
    own_place = own_spot * quarter + 1
    own_turn = 2 * own_spot + 1

    def place_of(zslot, spot):
        return (zslot // quarter) * half + spot * quarter + lax.rem(zslot, quarter)

    def copy_in(s):
        at = pl.ds(2 * s, 2)
        return (
            pltpu.make_async_copy(spec_hbm.at[at], spec.at[at], spec_sem.at[s]),
            pltpu.make_async_copy(leg_hbm.at[at], leg.at[at], leg_sem.at[s]),
        )

    wave_copy = pltpu.make_async_copy(wave_hbm, wave_smem, wave_sem)
    wave_copy.start()
    for copy in copy_in(0):
        copy.start()

    barrier = pltpu.get_barrier_semaphore()

    def greet(i, carry):
        pl.semaphore_signal(barrier, inc=1, device_id=(lev, lax.rem(me + i, devices)), device_id_type=MESH)
        return carry

    lax.fori_loop(1, devices, greet, 0)

    wave_copy.wait()
    lane_row = lax.broadcasted_iota(jnp.int32, (1, LANES), 1)
    own_waves = jnp.zeros((1, LANES), jnp.float32)
    for k in range(slots):
        own_waves = jnp.where(lane_row == k, wave_smem[k].astype(jnp.float32), own_waves)
    wave_recv[own_place] = own_waves

    degree = lax.broadcasted_iota(jnp.int32, (1, degrees), 1)

    def slot_sums(k):
        offset = degree - wave_smem[k]
        kept = jnp.where(offset >= 0, 1.0, 0.0)
        flipped = jnp.where((offset & 1) == 0, kept, -kept)
        rows_in = spec[k].astype(jnp.float32)
        both = jnp.concatenate([rows_in * kept, rows_in * flipped], 0).astype(jnp.bfloat16)
        return jnp.dot(both, leg[k], preferred_element_type=jnp.float32)

    def make_pair(s):
        first = slot_sums(2 * s)
        second = slot_sums(2 * s + 1)
        for side in range(2):
            low = side * columns
            stacked = jnp.concatenate([first[low : low + columns], second[low : low + columns]], 0)
            turned[side] = stacked.T
        group = 4

        def pack(g, carry):
            for side in range(2):
                piece = turned[side, pl.ds(pl.multiple_of(g * group * rows, 8), group * rows), :]
                for i in range(group):
                    send[s, side, g * group + i] = piece[i * rows : (i + 1) * rows]
            return carry

        lax.fori_loop(0, half // group, pack, 0)

    def own_block(to):
        return jnp.where(to >= half, 1, 0), jnp.where(to >= half, devices - 1 - to, to)

    def send_pair(s):
        def one(n, carry):
            turn = jnp.where(n >= own_turn, n + 1, n)
            far, rest = turn // (2 * plane), lax.rem(turn, 2 * plane)
            zslot, spot = 2 * far + lax.rem(rest, 2), rest // 2
            dy, dx = in_plane(spot)
            to = device_at(along_z(zslot), dy, dx)
            side, block = own_block(to)
            part = zslot // quarter
            pltpu.make_async_remote_copy(
                src_ref=send.at[s, side, block],
                dst_ref=recv.at[s, place_of(zslot, spot)],
                send_sem=send_sem.at[s],
                recv_sem=recv_sem.at[s, part],
                device_id=(lev, to),
                device_id_type=MESH,
            ).start()
            return carry

        lax.fori_loop(0, devices - 1, one, 0)
        side, block = own_block(me)
        pltpu.make_async_copy(send.at[s, side, block], recv.at[s, own_place], recv_sem.at[s, 0]).start()

    for copy in copy_in(0):
        copy.wait()
    for s in range(1, pairs):
        for copy in copy_in(s):
            copy.start()
    make_pair(0)
    out_ref[...] = jnp.zeros_like(out_ref)
    pl.semaphore_wait(barrier, devices - 1)

    def send_line(n, carry):
        zslot = jnp.where(n >= 1, n + 1, n)
        pltpu.make_async_remote_copy(
            src_ref=wave_recv.at[own_place],
            dst_ref=wave_recv.at[place_of(zslot, own_spot)],
            send_sem=line_send_sem,
            recv_sem=line_recv_sem,
            device_id=(lev, device_at(along_z(zslot), 0, 0)),
            device_id_type=MESH,
        ).start()
        return carry

    lax.fori_loop(0, size_z - 1, send_line, 0)
    send_pair(0)

    line_rows = wave_recv.at[pl.ds(0, size_z - 1)]
    pltpu.make_async_copy(line_rows, line_rows, line_recv_sem).wait()

    def send_plane(n, carry):
        spot = jnp.where(n >= own_spot, n + 1, n)
        dy, dx = in_plane(spot)
        for part in range(2):
            pltpu.make_async_remote_copy(
                src_ref=wave_recv.at[pl.ds(part * half + own_spot * quarter, quarter)],
                dst_ref=wave_recv.at[pl.ds(part * half + spot * quarter, quarter)],
                send_sem=plane_send_sem,
                recv_sem=plane_recv_sem,
                device_id=(lev, device_at(0, dy, dx)),
                device_id_type=MESH,
            ).start()
        return carry

    lax.fori_loop(0, plane - 1, send_plane, 0)

    def later_pair(s, carry):
        for copy in copy_in(s):
            copy.wait()
        make_pair(s)
        send_pair(s)
        return carry

    lax.fori_loop(1, pairs, later_pair, 0)

    plane_rows = wave_recv.at[pl.ds(0, size_z * (plane - 1))]
    pltpu.make_async_copy(plane_rows, plane_rows, plane_recv_sem).wait()

    waves = wave_recv[:, 0, :]
    step_units = waves - 20.0 * jnp.floor((waves + 0.5) * 0.05)
    step_angle = step_units * (2.0 * math.pi / 20.0)
    wave_trig[0] = waves
    wave_trig[1] = jnp.cos(step_angle)
    wave_trig[2] = jnp.sin(step_angle)
    lane_id = lax.broadcasted_iota(jnp.int32, (half, LANES), 1)
    lane_number = lane_id.astype(jnp.float32)

    def make_tables(s, part):
        first_row = pl.multiple_of(part * half, half)

        def column(which, k):
            picked = jnp.where(lane_id == k, wave_trig[which, pl.ds(first_row, half), :], 0.0)
            return jnp.broadcast_to(jnp.sum(picked, axis=1, keepdims=True), (half, LANES))

        for t in range(2):
            k = 2 * s + t
            wave = column(0, k)
            cos_step = column(1, k)
            sin_step = column(2, k)
            product = wave * lane_number
            turns = jnp.floor(product * (1.0 / NLON) + 0.5)
            angle = (product - turns * NLON) * (2.0 * math.pi / NLON)
            weight = jnp.where(wave == 0.0, 1.0, 2.0)
            cos_part = weight * jnp.cos(angle)
            sin_part = -weight * jnp.sin(angle)
            for q in range(NLON // LANES):
                at = slice(q * LANES, (q + 1) * LANES)
                for p, now in ((0, cos_part), (1, sin_part)):
                    low = (2 * t + p) * half
                    high_bits = now.astype(jnp.bfloat16)
                    table_hi[low : low + half, at] = high_bits
                    table_lo[low : low + half, at] = (now - high_bits.astype(jnp.float32)).astype(jnp.bfloat16)
                cos_part, sin_part = (
                    cos_part * cos_step + sin_part * sin_step,
                    sin_part * cos_step - cos_part * sin_step,
                )

    all_rows = rows * levels

    def use_part(s, part):
        for r in range(rows):
            tile = recv[s, pl.ds(part * half, half), r, :].T
            at = pl.multiple_of(jnp.where(me >= half, rows - 1 - r, r) * levels, levels)
            for t in range(2):
                low = 2 * t * levels
                piece = jnp.concatenate([tile[low : low + levels], tile[low + levels : low + 2 * levels]], 1)
                high_bits = piece.astype(jnp.bfloat16)
                low_bits = (piece - high_bits.astype(jnp.float32)).astype(jnp.bfloat16)
                across = slice(t * 2 * half, (t + 1) * 2 * half)
                xs[pl.ds(at, levels), across] = high_bits
                xs[pl.ds(at + all_rows, levels), across] = low_bits
        width = 512

        def block(j, carry):
            at = pl.ds(pl.multiple_of(j * width, width), width)
            main = jnp.dot(xs[...], table_hi[:, at], preferred_element_type=jnp.float32)
            rest = jnp.dot(xs[0:all_rows], table_lo[:, at], preferred_element_type=jnp.float32)
            out_ref[:, at] += main[0:all_rows] + (main[all_rows:] + rest)
            return carry

        lax.fori_loop(0, NLON // width, block, 0)

    def arrive(u, carry):
        s, part = u // 2, lax.rem(u, 2)
        make_tables(s, part)
        arrived = recv.at[s, pl.ds(part * half, half)]
        pltpu.make_async_copy(arrived, arrived, recv_sem.at[s, part]).wait()
        use_part(s, part)
        return carry

    def finish(s, carry):
        sent = recv.at[s, pl.ds(0, devices - 1)]
        pltpu.make_async_copy(sent, sent, send_sem.at[s]).wait()
        return carry

    lax.fori_loop(0, 2 * pairs, arrive, 0)
    lax.fori_loop(0, pairs, finish, 0)
    pltpu.make_async_copy(line_rows, line_rows, line_send_sem).wait()
    pltpu.make_async_copy(plane_rows, plane_rows, plane_send_sem).wait()


def solution(mesh):
    devices = mesh.shape["wa"]

    def on_device(spectral, legendre, wavenumber):
        slots, degrees, parts, levels = spectral.shape
        north = legendre.shape[2]
        columns = parts * levels
        rows = 2 * north // devices
        pairs = slots // 2
        half = devices // 2
        spec_rows = jnp.transpose(spectral, (0, 2, 3, 1)).reshape(slots, columns, degrees)
        dims = (SIZES, slots, degrees, north, columns, rows)
        gridded = pl.pallas_call(
            functools.partial(kernel, dims),
            out_shape=jax.ShapeDtypeStruct((rows * levels, NLON), jnp.float32),
            in_specs=[
                pl.BlockSpec(memory_space=pltpu.HBM),
                pl.BlockSpec(memory_space=pltpu.HBM),
                pl.BlockSpec(memory_space=pltpu.HBM),
            ],
            out_specs=pl.BlockSpec(memory_space=pltpu.VMEM),
            scratch_shapes=[
                pltpu.VMEM((slots, columns, degrees), jnp.bfloat16),
                pltpu.VMEM((slots, degrees, north), jnp.bfloat16),
                pltpu.VMEM((2, north, LANES), jnp.float32),
                pltpu.VMEM((pairs, 2, half, rows, LANES), jnp.float32),
                pltpu.VMEM((pairs, devices, rows, LANES), jnp.float32),
                pltpu.SMEM((slots,), jnp.int32),
                pltpu.VMEM((devices, 1, LANES), jnp.float32),
                pltpu.VMEM((3, devices, LANES), jnp.float32),
                pltpu.VMEM((4 * half, NLON), jnp.bfloat16),
                pltpu.VMEM((4 * half, NLON), jnp.bfloat16),
                pltpu.VMEM((2 * rows * levels, 4 * half), jnp.bfloat16),
                pltpu.SemaphoreType.DMA,
                pltpu.SemaphoreType.DMA((pairs,)),
                pltpu.SemaphoreType.DMA((pairs,)),
                pltpu.SemaphoreType.DMA,
                pltpu.SemaphoreType.DMA,
                pltpu.SemaphoreType.DMA,
                pltpu.SemaphoreType.DMA,
                pltpu.SemaphoreType.DMA((pairs,)),
                pltpu.SemaphoreType.DMA((pairs, 2)),
            ],
            compiler_params=pltpu.CompilerParams(
                collective_id=0, has_side_effects=True, vmem_limit_bytes=48 * 2**20
            ),
        )(
            pltpu.with_memory_space_constraint(spec_rows, pltpu.HBM),
            pltpu.with_memory_space_constraint(legendre, pltpu.HBM),
            pltpu.with_memory_space_constraint(wavenumber, pltpu.HBM),
        )
        return jnp.transpose(gridded.reshape(rows, levels, NLON), (0, 2, 1))

    return jax.shard_map(
        on_device,
        mesh=mesh,
        in_specs=(P("wa", None, None, "lev"), P("wa", None, None), P("wa")),
        out_specs=P("wa", None, "lev"),
        check_vma=False,
    )
```

time: 68.8 us -> 80.1 us (1.16)
  Pallas kernels: 65.7 us -> 78.8 us
  local copies, waits for them, and re-layouts: 2.99 us -> 1.27 us
    pallas_call x1, Pallas kernels: 65.7 us -> 78.8 us  [on_device(): pl.pallas_call(functools.partial(kernel, dims), out_shape=jax.ShapeDtypeS...]
    unnamed x1, local copies, waits for them, and re-layouts: 2.99 us -> 1.27 us
where the time goes in v2:
time: 80.1 us
  Pallas kernels  78.8 us (98%)
  local copies, waits for them, and re-layouts  1.27 us (2%)
    pallas_call x1, Pallas kernels, on_device(): pl.pallas_call(functools.partial(kernel, dims), out_shape=jax.ShapeDtypeS...  78.8 us

profile of v2, /device:TPU:1, one launch (start us, length us, event | category | flops | bytes accessed | tf_op | source)
XLA Modules:
  0.0 80.1 jit_solution(7438951660720164215)
XLA Ops:
  0.0 78.8 %shard_map.37 = f32[192,2560]{1,0:T(8,128)S(1)} custom-call(bf16[10,64,1280]{2,1,0:T(8,128)(2,1)} %bitcast.7, bf16[10,1280,384]{2,1,0:T(8,128)(2,1)} %leg_hbm.1, s32[10]{0:T(128)} %wave_hbm.1), custom_call_target="tpu_custom_call" | custom-call | tf_op jit(solution)/shard_map/pallas_call | solution.py:310
  78.8 1.3 %copy.5 = f32[6,2560,32]{1,2,0:T(8,128)} copy(f32[6,2560,32]{1,2,0:T(8,128)S(1)} %bitcast.6) | data formatting | bytes 3932160

commit v3 on v2

--- a/solution.py
+++ b/solution.py
@@ -11,7 +11,9 @@
 NLON = 2560
 LANES = 128
 MESH = pl.DeviceIdType.MESH
-SIZES = (4, 8, 4)
+STEP = 4
+LINE = 8
+LINE_ORDER = (4, 3, 5, 2, 6, 1, 7, 0)
 
 
 def kernel(
@@ -41,40 +43,26 @@
     send_sem,
     recv_sem,
 ):
-    sizes, slots, degrees, north, columns, rows = dims
-    size_y, size_z, size_x = sizes
-    devices = size_y * size_z * size_x
-    plane = size_y * size_x
-    quarter = size_z // 2
+    devices, slots, degrees, north, columns, rows = dims
     pairs = slots // 2
     half = devices // 2
+    groups = devices // LINE
     levels = columns // 2
     lev = lax.axis_index("lev")
     me = lax.axis_index("wa")
-    my_y = me // (size_z * size_x)
-    my_z = lax.rem(me // size_x, size_z)
-    my_x = lax.rem(me, size_x)
-
-    def along_z(zslot):
-        far, low = zslot // 2, lax.rem(zslot, 2)
-        return jnp.where(low == 0, size_z // 2 - far, jnp.where(far == 0, 0, size_z // 2 + far))
-
-    def in_plane(spot):
-        dy = lax.rem(size_y // 2 + (size_y - 1) * (spot // size_x), size_y)
-        dx = lax.rem(size_x // 2 + (size_x - 1) * lax.rem(spot, size_x), size_x)
-        return dy, dx
-
-    def device_at(dz, dy, dx):
-        return (
-            lax.rem(my_y + dy, size_y) * size_z + lax.rem(my_z + dz, size_z)
-        ) * size_x + lax.rem(my_x + dx, size_x)
-
-    own_spot = (size_y // 2) * size_x + size_x // 2
-    own_place = own_spot * quarter + 1
-    own_turn = 2 * own_spot + 1
-
-    def place_of(zslot, spot):
-        return (zslot // quarter) * half + spot * quarter + lax.rem(zslot, quarter)
+
+    def target(m, k):
+        return (me + (m // STEP * (LINE * STEP) + m % STEP + k * STEP)) & (devices - 1)
+
+    def copy_row(src, dst, sends, receives, to):
+        pltpu.make_async_remote_copy(
+            src_ref=src,
+            dst_ref=dst,
+            send_sem=sends,
+            recv_sem=receives,
+            device_id=(lev, to),
+            device_id_type=MESH,
+        ).start()
 
     def copy_in(s):
         at = pl.ds(2 * s, 2)
@@ -90,18 +78,26 @@
 
     barrier = pltpu.get_barrier_semaphore()
 
-    def greet(i, carry):
-        pl.semaphore_signal(barrier, inc=1, device_id=(lev, lax.rem(me + i, devices)), device_id_type=MESH)
-        return carry
-
-    lax.fori_loop(1, devices, greet, 0)
+    def greet(m, first):
+        for k in range(first, LINE):
+            pl.semaphore_signal(
+                barrier, inc=1, device_id=(lev, (me + m * LINE + k) & (devices - 1)), device_id_type=MESH
+            )
+
+    greet(0, 1)
+
+    def greet_line(m, carry):
+        greet(m, 0)
+        return carry
+
+    lax.fori_loop(1, groups, greet_line, 0)
 
     wave_copy.wait()
     lane_row = lax.broadcasted_iota(jnp.int32, (1, LANES), 1)
     own_waves = jnp.zeros((1, LANES), jnp.float32)
     for k in range(slots):
         own_waves = jnp.where(lane_row == k, wave_smem[k].astype(jnp.float32), own_waves)
-    wave_recv[own_place] = own_waves
+    wave_recv[0] = own_waves
 
     degree = lax.broadcasted_iota(jnp.int32, (1, degrees), 1)
 
@@ -126,36 +122,28 @@
             for side in range(2):
                 piece = turned[side, pl.ds(pl.multiple_of(g * group * rows, 8), group * rows), :]
                 for i in range(group):
-                    send[s, side, g * group + i] = piece[i * rows : (i + 1) * rows]
+                    band = g * group + i
+                    send[s, devices - 1 - band if side else band] = piece[i * rows : (i + 1) * rows]
             return carry
 
         lax.fori_loop(0, half // group, pack, 0)
 
-    def own_block(to):
-        return jnp.where(to >= half, 1, 0), jnp.where(to >= half, devices - 1 - to, to)
+    def send_group(s, m, part, first):
+        for k in LINE_ORDER:
+            if k >= first:
+                to = target(m, k)
+                copy_row(send.at[s, to], recv.at[s, m * LINE + k], send_sem.at[s], recv_sem.at[s, part], to)
 
     def send_pair(s):
-        def one(n, carry):
-            turn = jnp.where(n >= own_turn, n + 1, n)
-            far, rest = turn // (2 * plane), lax.rem(turn, 2 * plane)
-            zslot, spot = 2 * far + lax.rem(rest, 2), rest // 2
-            dy, dx = in_plane(spot)
-            to = device_at(along_z(zslot), dy, dx)
-            side, block = own_block(to)
-            part = zslot // quarter
-            pltpu.make_async_remote_copy(
-                src_ref=send.at[s, side, block],
-                dst_ref=recv.at[s, place_of(zslot, spot)],
-                send_sem=send_sem.at[s],
-                recv_sem=recv_sem.at[s, part],
-                device_id=(lev, to),
-                device_id_type=MESH,
-            ).start()
-            return carry
-
-        lax.fori_loop(0, devices - 1, one, 0)
-        side, block = own_block(me)
-        pltpu.make_async_copy(send.at[s, side, block], recv.at[s, own_place], recv_sem.at[s, 0]).start()
+        send_group(s, 0, 0, 1)
+        for part in range(2):
+
+            def one(m, carry):
+                send_group(s, m, part, 0)
+                return carry
+
+            lax.fori_loop(max(1, part * groups // 2), (part + 1) * groups // 2, one, 0)
+        pltpu.make_async_copy(send.at[s, me], recv.at[s, 0], recv_sem.at[s, 0]).start()
 
     for copy in copy_in(0):
         copy.wait()
@@ -166,39 +154,19 @@
     out_ref[...] = jnp.zeros_like(out_ref)
     pl.semaphore_wait(barrier, devices - 1)
 
-    def send_line(n, carry):
-        zslot = jnp.where(n >= 1, n + 1, n)
-        pltpu.make_async_remote_copy(
-            src_ref=wave_recv.at[own_place],
-            dst_ref=wave_recv.at[place_of(zslot, own_spot)],
-            send_sem=line_send_sem,
-            recv_sem=line_recv_sem,
-            device_id=(lev, device_at(along_z(zslot), 0, 0)),
-            device_id_type=MESH,
-        ).start()
-        return carry
-
-    lax.fori_loop(0, size_z - 1, send_line, 0)
+    for k in range(1, LINE):
+        copy_row(wave_recv.at[0], wave_recv.at[k], line_send_sem, line_recv_sem, target(0, k))
     send_pair(0)
 
-    line_rows = wave_recv.at[pl.ds(0, size_z - 1)]
+    line_rows = wave_recv.at[pl.ds(0, LINE - 1)]
     pltpu.make_async_copy(line_rows, line_rows, line_recv_sem).wait()
 
-    def send_plane(n, carry):
-        spot = jnp.where(n >= own_spot, n + 1, n)
-        dy, dx = in_plane(spot)
-        for part in range(2):
-            pltpu.make_async_remote_copy(
-                src_ref=wave_recv.at[pl.ds(part * half + own_spot * quarter, quarter)],
-                dst_ref=wave_recv.at[pl.ds(part * half + spot * quarter, quarter)],
-                send_sem=plane_send_sem,
-                recv_sem=plane_recv_sem,
-                device_id=(lev, device_at(0, dy, dx)),
-                device_id_type=MESH,
-            ).start()
-        return carry
-
-    lax.fori_loop(0, plane - 1, send_plane, 0)
+    def send_plane(m, carry):
+        rows_out = wave_recv.at[pl.ds(m * LINE, LINE)]
+        copy_row(wave_recv.at[pl.ds(0, LINE)], rows_out, plane_send_sem, plane_recv_sem, target(m, 0))
+        return carry
+
+    lax.fori_loop(1, groups, send_plane, 0)
 
     def later_pair(s, carry):
         for copy in copy_in(s):
@@ -209,7 +177,7 @@
 
     lax.fori_loop(1, pairs, later_pair, 0)
 
-    plane_rows = wave_recv.at[pl.ds(0, size_z * (plane - 1))]
+    plane_rows = wave_recv.at[pl.ds(0, devices - LINE)]
     pltpu.make_async_copy(plane_rows, plane_rows, plane_recv_sem).wait()
 
     waves = wave_recv[:, 0, :]
@@ -306,7 +274,7 @@
         pairs = slots // 2
         half = devices // 2
         spec_rows = jnp.transpose(spectral, (0, 2, 3, 1)).reshape(slots, columns, degrees)
-        dims = (SIZES, slots, degrees, north, columns, rows)
+        dims = (devices, slots, degrees, north, columns, rows)
         gridded = pl.pallas_call(
             functools.partial(kernel, dims),
             out_shape=jax.ShapeDtypeStruct((rows * levels, NLON), jnp.float32),
@@ -320,7 +288,7 @@
                 pltpu.VMEM((slots, columns, degrees), jnp.bfloat16),
                 pltpu.VMEM((slots, degrees, north), jnp.bfloat16),
                 pltpu.VMEM((2, north, LANES), jnp.float32),
-                pltpu.VMEM((pairs, 2, half, rows, LANES), jnp.float32),
+                pltpu.VMEM((pairs, devices, rows, LANES), jnp.float32),
                 pltpu.VMEM((pairs, devices, rows, LANES), jnp.float32),
                 pltpu.SMEM((slots,), jnp.int32),
                 pltpu.VMEM((devices, 1, LANES), jnp.float32),

time: 80.1 us -> 61.8 us (0.77); the launches traced: 80.1 us -> 60.6 us
  Pallas kernels: 78.8 us -> 59.3 us
    pallas_call x1, Pallas kernels: 78.8 us -> 59.3 us  [on_device(): pl.pallas_call(functools.partial(kernel, dims), out_shape=jax.ShapeDtypeS...]
where the time goes in v3:
time: 61.8 us; the launch traced here: 60.6 us
  Pallas kernels  59.3 us (96%)
  local copies, waits for them, and re-layouts  1.27 us (2%)
    pallas_call x1, Pallas kernels, on_device(): pl.pallas_call(functools.partial(kernel, dims), out_shape=jax.ShapeDtypeS...  59.3 us
    unnamed x1, local copies, waits for them, and re-layouts  1.27 us

profile of v3, /device:TPU:1, one launch (start us, length us, event | category | flops | bytes accessed | tf_op | source)
XLA Modules:
  0.0 60.6 jit_solution(12310983511185287015)
XLA Ops:
  0.0 59.3 %shard_map.37 = f32[192,2560]{1,0:T(8,128)S(1)} custom-call(bf16[10,64,1280]{2,1,0:T(8,128)(2,1)} %bitcast.7, bf16[10,1280,384]{2,1,0:T(8,128)(2,1)} %leg_hbm.1, s32[10]{0:T(128)} %wave_hbm.1), custom_call_target="tpu_custom_call" | custom-call | tf_op jit(solution)/shard_map/pallas_call | solution.py:278
  59.3 1.3 %copy.5 = f32[6,2560,32]{1,2,0:T(8,128)} copy(f32[6,2560,32]{1,2,0:T(8,128)S(1)} %bitcast.6) | data formatting | bytes 3932160

commit v4 on v3

--- a/solution.py
+++ b/solution.py
@@ -30,8 +30,8 @@
     wave_smem,
     wave_recv,
     wave_trig,
-    table_hi,
-    table_lo,
+    table,
+    sign,
     xs,
     wave_sem,
     spec_sem,
@@ -186,8 +186,12 @@
     wave_trig[0] = waves
     wave_trig[1] = jnp.cos(step_angle)
     wave_trig[2] = jnp.sin(step_angle)
+    wave_trig[3] = 1.0 - 2.0 * (waves - 2.0 * jnp.floor(waves * 0.5))
     lane_id = lax.broadcasted_iota(jnp.int32, (half, LANES), 1)
     lane_number = lane_id.astype(jnp.float32)
+
+    all_rows = rows * levels
+    deep = 4 * half
 
     def make_tables(s, part):
         first_row = pl.multiple_of(part * half, half)
@@ -196,6 +200,8 @@
             picked = jnp.where(lane_id == k, wave_trig[which, pl.ds(first_row, half), :], 0.0)
             return jnp.broadcast_to(jnp.sum(picked, axis=1, keepdims=True), (half, LANES))
 
+        signs = jnp.where(lane_id < LANES // 2, column(3, 2 * s), column(3, 2 * s + 1))
+        sign[...] = signs.T
         for t in range(2):
             k = 2 * s + t
             wave = column(0, k)
@@ -207,19 +213,19 @@
             weight = jnp.where(wave == 0.0, 1.0, 2.0)
             cos_part = weight * jnp.cos(angle)
             sin_part = -weight * jnp.sin(angle)
-            for q in range(NLON // LANES):
+            for q in range(NLON // 2 // LANES):
                 at = slice(q * LANES, (q + 1) * LANES)
                 for p, now in ((0, cos_part), (1, sin_part)):
                     low = (2 * t + p) * half
                     high_bits = now.astype(jnp.bfloat16)
-                    table_hi[low : low + half, at] = high_bits
-                    table_lo[low : low + half, at] = (now - high_bits.astype(jnp.float32)).astype(jnp.bfloat16)
+                    low_bits = (now - high_bits.astype(jnp.float32)).astype(jnp.bfloat16)
+                    table[low : low + half, at] = high_bits
+                    table[deep + low : deep + low + half, at] = low_bits
                 cos_part, sin_part = (
                     cos_part * cos_step + sin_part * sin_step,
                     sin_part * cos_step - cos_part * sin_step,
                 )
 
-    all_rows = rows * levels
 
     def use_part(s, part):
         for r in range(rows):
@@ -230,19 +236,16 @@
                 piece = jnp.concatenate([tile[low : low + levels], tile[low + levels : low + 2 * levels]], 1)
                 high_bits = piece.astype(jnp.bfloat16)
                 low_bits = (piece - high_bits.astype(jnp.float32)).astype(jnp.bfloat16)
-                across = slice(t * 2 * half, (t + 1) * 2 * half)
-                xs[pl.ds(at, levels), across] = high_bits
-                xs[pl.ds(at + all_rows, levels), across] = low_bits
-        width = 512
-
-        def block(j, carry):
-            at = pl.ds(pl.multiple_of(j * width, width), width)
-            main = jnp.dot(xs[...], table_hi[:, at], preferred_element_type=jnp.float32)
-            rest = jnp.dot(xs[0:all_rows], table_lo[:, at], preferred_element_type=jnp.float32)
-            out_ref[:, at] += main[0:all_rows] + (main[all_rows:] + rest)
-            return carry
-
-        lax.fori_loop(0, NLON // width, block, 0)
+                turn = sign[low : low + levels].astype(jnp.bfloat16)
+                turn = jnp.concatenate([turn, turn], 1)
+                for i, bits in enumerate((high_bits, high_bits, low_bits)):
+                    across = slice(i * deep + t * 2 * half, i * deep + (t + 1) * 2 * half)
+                    xs[pl.ds(at, levels), across] = bits
+                    xs[pl.ds(at + all_rows, levels), across] = bits * turn
+        total = jnp.dot(xs[:, 0 : 2 * deep], table[...], preferred_element_type=jnp.float32)
+        total += jnp.dot(xs[:, 2 * deep :], table[0:deep], preferred_element_type=jnp.float32)
+        out_ref[:, 0 : NLON // 2] += total[0:all_rows]
+        out_ref[:, NLON // 2 :] += total[all_rows:]
 
     def arrive(u, carry):
         s, part = u // 2, lax.rem(u, 2)
@@ -292,10 +295,10 @@
                 pltpu.VMEM((pairs, devices, rows, LANES), jnp.float32),
                 pltpu.SMEM((slots,), jnp.int32),
                 pltpu.VMEM((devices, 1, LANES), jnp.float32),
-                pltpu.VMEM((3, devices, LANES), jnp.float32),
-                pltpu.VMEM((4 * half, NLON), jnp.bfloat16),
-                pltpu.VMEM((4 * half, NLON), jnp.bfloat16),
-                pltpu.VMEM((2 * rows * levels, 4 * half), jnp.bfloat16),
+                pltpu.VMEM((4, devices, LANES), jnp.float32),
+                pltpu.VMEM((8 * half, NLON // 2), jnp.bfloat16),
+                pltpu.VMEM((LANES, half), jnp.float32),
+                pltpu.VMEM((2 * rows * levels, 12 * half), jnp.bfloat16),
                 pltpu.SemaphoreType.DMA,
                 pltpu.SemaphoreType.DMA((pairs,)),
                 pltpu.SemaphoreType.DMA((pairs,)),

time: 61.8 us -> 60.1 us (0.972); the launches traced: 60.6 us -> 59.9 us
  Pallas kernels: 59.3 us -> 58.6 us
    pallas_call x1, Pallas kernels: 59.3 us -> 58.6 us  [on_device(): pl.pallas_call(functools.partial(kernel, dims), out_shape=jax.ShapeDtypeS...]
where the time goes in v4:
time: 60.1 us; the launch traced here: 59.9 us
  Pallas kernels  58.6 us (98%)
  local copies, waits for them, and re-layouts  1.27 us (2%)
    pallas_call x1, Pallas kernels, on_device(): pl.pallas_call(functools.partial(kernel, dims), out_shape=jax.ShapeDtypeS...  58.6 us
    unnamed x1, local copies, waits for them, and re-layouts  1.27 us

profile of v4, /device:TPU:1, one launch (start us, length us, event | category | flops | bytes accessed | tf_op | source)
XLA Modules:
  0.0 59.9 jit_solution(4059057735163798869)
XLA Ops:
  0.0 58.6 %shard_map.37 = f32[192,2560]{1,0:T(8,128)S(1)} custom-call(bf16[10,64,1280]{2,1,0:T(8,128)(2,1)} %bitcast.7, bf16[10,1280,384]{2,1,0:T(8,128)(2,1)} %leg_hbm.1, s32[10]{0:T(128)} %wave_hbm.1), custom_call_target="tpu_custom_call" | custom-call | tf_op jit(solution)/shard_map/pallas_call | solution.py:281
  58.6 1.3 %copy.5 = f32[6,2560,32]{1,2,0:T(8,128)} copy(f32[6,2560,32]{1,2,0:T(8,128)S(1)} %bitcast.6) | data formatting | bytes 3932160
